TPU v7x, 128 devices: a whole 4x4x4 slice. The times are simulated.
128 devices in a mesh: section: 8 (over x, y_lo), seq: 16 (over z, y_hi, core).
Axes of the slice: x: 4, y: 4 (y_hi: 2, y_lo: 2; y = y_hi * 2 + y_lo), z: 4, core: 2. Of those that a mesh axis runs over, the one named last changes fastest.
Arguments:
- queries: bfloat16 [8, 2048, 4096], P('section', 'seq'), may hold values from -500 to 500
- keys: bfloat16 [8, 2048, 512], P('section', 'seq'), may hold values from -6 to 6
- values: bfloat16 [8, 2048, 512], P('section', 'seq'), may hold values from -6 to 6
- out_grad: bfloat16 [8, 2048, 4096], P('section', 'seq'), may hold values from -6 to 6
- documents: int32 [8, 2048], P('section'), may hold values from 0 to 3, never falling along the last dimension, each value on 1 to 1024 neighbouring positions
- query_weight: bfloat16 [8, 4096, 4096], P('section', 'seq'), may hold values from -0.09375 to 0.09375
- key_weight: bfloat16 [8, 512, 4096], P('section'), may hold values from -0.125 to 0.125
- value_weight: bfloat16 [8, 512, 4096], P('section'), may hold values from -0.125 to 0.125
Outputs:
- upstream: bfloat16 [8, 2048, 4096], P('section', 'seq')
Inputs may be any that keep to these rules, and one draw needn't show every extreme that they name: `documents`: each section's document ids never fall along its tokens.
All inputs are finite; a program needn't handle non-finite values.
Results may differ from a plain program's by a relative error of at most 0.0058.
Values may be sent and summed in bfloat16 or wider, within the bound.
A program may use at most 192 MiB of HBM per device.

v0:
```python
import math

import jax
import jax.numpy as jnp
from jax import lax
from jax.sharding import PartitionSpec as P

H = 32
KV = 4
HD = 128


def side_by_side(arrays, axis, split_dim, concat_dim, along):
    ends, at = ([], 0)
    for a in arrays[:-1]:
        at += a.shape[along]
        ends.append(at)
    both = jnp.concatenate(arrays, axis=along)
    return tuple(
        jnp.split(
            lax.all_to_all(both, axis, split_axis=split_dim, concat_axis=concat_dim, tiled=True),
            ends,
            axis=along,
        )
    )


def sent_together(arrays, axis, dim, along):
    widths = [a.shape[along] for a in arrays]
    both = jnp.concatenate(arrays, axis=along)
    result = lax.all_gather(both, axis, axis=dim, tiled=True)
    return tuple(jnp.split(result, [sum(widths[:k]) for k in range(1, len(widths))], axis=along))


def passed_along(block, axis, distance):
    devices = range(lax.axis_size(axis))
    route = [(i - distance, i) for i in devices if i - distance in devices]
    return lax.ppermute(block, axis, route)


def body(queries, keys, values, out_grad, documents, query_weight, key_weight, value_weight):
    count = lax.axis_size("seq")
    myself = lax.axis_index("seq")
    tok = queries.shape[1]
    total = tok * count
    heads_here = query_weight.shape[1] // HD
    group = H // KV
    reps = count // KV
    scale = 1.0 / math.sqrt(HD)
    kv_head = myself * heads_here // group
    q_send = queries[0].reshape(tok, count, heads_here * HD)
    o_send = out_grad[0].reshape(tok, count, heads_here * HD)
    q_all, o_all = side_by_side((q_send, o_send), "seq", 1, 0, 2)
    q_all = q_all.reshape(total, heads_here, HD)
    o_all = o_all.reshape(total, heads_here, HD)
    k_whole, v_whole = sent_together((keys[0], values[0]), "seq", 0, 1)
    k_head = lax.dynamic_slice_in_dim(k_whole, kv_head * HD, HD, 1)
    v_head = lax.dynamic_slice_in_dim(v_whole, kv_head * HD, HD, 1)
    doc_ids = documents[0]
    block = min(512, total)
    columns = lax.iota(jnp.int32, total)

    def attend(carry, index):
        dkey, dvalue = carry
        first = index * block
        q_blk = lax.dynamic_slice_in_dim(q_all, first, block, 0)
        o_blk = lax.dynamic_slice_in_dim(o_all, first, block, 0)
        rows = first + lax.iota(jnp.int32, block)
        row_ids = lax.dynamic_slice_in_dim(doc_ids, first, block, 0)
        allowed = (columns[None, :] <= rows[:, None]) & (doc_ids[None, :] == row_ids[:, None])
        scores = (
            jnp.einsum("bhd,td->hbt", q_blk, k_head, preferred_element_type=jnp.float32) * scale
        )
        scores = jnp.where(allowed[None], scores, -jnp.inf)
        top = jnp.max(scores, axis=-1, keepdims=True)
        expo = jnp.exp(scores - top)
        prob = expo / jnp.sum(expo, axis=-1, keepdims=True)
        prob_low = prob.astype(jnp.bfloat16)
        dprob = jnp.einsum("bhd,td->hbt", o_blk, v_head, preferred_element_type=jnp.float32)
        delta = jnp.sum(prob * dprob, axis=-1, keepdims=True)
        dscore = (prob * (dprob - delta) * scale).astype(jnp.bfloat16)
        dq_blk = jnp.einsum(
            "hbt,td->bhd", dscore, k_head, preferred_element_type=jnp.float32
        ).astype(jnp.bfloat16)
        dkey = dkey + jnp.einsum("hbt,bhd->td", dscore, q_blk, preferred_element_type=jnp.float32)
        dvalue = dvalue + jnp.einsum(
            "hbt,bhd->td", prob_low, o_blk, preferred_element_type=jnp.float32
        )
        return ((dkey, dvalue), dq_blk)

    start_carry = (jnp.zeros((total, HD), jnp.float32), jnp.zeros((total, HD), jnp.float32))
    (dkey, dvalue), dq_blocks = lax.scan(
        attend, start_carry, jnp.arange(total // block, dtype=jnp.int32)
    )
    dquery = dq_blocks.reshape(total, heads_here * HD)
    dkey_low = dkey.astype(jnp.bfloat16)
    dvalue_low = dvalue.astype(jnp.bfloat16)
    dq_tok, dk_tok, dv_tok = side_by_side(
        (
            dquery.reshape(total, 1, heads_here * HD),
            dkey_low.reshape(total, 1, HD),
            dvalue_low.reshape(total, 1, HD),
        ),
        "seq",
        0,
        1,
        2,
    )
    dq_tok = dq_tok.reshape(tok, count * heads_here * HD)
    dk_tok = dk_tok.reshape(tok, count * HD)
    dv_tok = dv_tok.reshape(tok, count * HD)
    wk_rep = jnp.repeat(key_weight[0].reshape(KV, HD, -1), reps, axis=0).reshape(count * HD, -1)
    wv_rep = jnp.repeat(value_weight[0].reshape(KV, HD, -1), reps, axis=0).reshape(count * HD, -1)
    start_sum = jnp.dot(dk_tok, wk_rep, preferred_element_type=jnp.float32)
    start_sum = start_sum + jnp.dot(dv_tok, wv_rep, preferred_element_type=jnp.float32)
    dinput = start_sum + jnp.dot(
        dq_tok,
        lax.all_gather(query_weight[0], "seq", axis=0, tiled=True),
        preferred_element_type=jnp.float32,
    )
    dinput = dinput.astype(jnp.bfloat16)
    received = passed_along(dinput, "section", -1)
    return received[None]


def solution(mesh):
    in_specs = (
        P("section", "seq", None),
        P("section", "seq", None),
        P("section", "seq", None),
        P("section", "seq", None),
        P("section", None),
        P("section", "seq", None),
        P("section", None, None),
        P("section", None, None),
    )
    out_specs = P("section", "seq", None)
    return jax.shard_map(body, mesh=mesh, in_specs=in_specs, out_specs=out_specs, check_vma=False)
```

profile of v0, /device:TPU:8, one launch (start us, length us, event | category | flops | bytes accessed | tf_op | source)
XLA Modules:
  0.0 405.7 jit_solution(12301831446187139007)
XLA Ops:
  6.5 1.7 pad_maximum_fusion.2
  8.3 0.7 all-gather.6.cloned.1.call-update
  9.0 1.6 copy.38
  10.6 1.6 copy.39
  12.3 1.4 pad_maximum_fusion
  13.7 7.1 %all-to-all-start = ((bf16[128,16,512]{0,2,1:T(8,128)(2,1)}), bf16[128,16,512]{0,2,1:T(8,128)(2,1)S(1)}, u32[]{:S(2)}, u32[]{:S(2)}) async-start(bf16[128,16,512]{0,2,1:T(8,128)(2,1)} %pad_maximum_fusion), calls=%async_computation | async-start | bytes 4194304 | tf_op jit(solution)/shard_map/all_to_all | solution.py:21
  20.9 32.0 %all-to-all-done = bf16[128,16,512]{0,2,1:T(8,128)(2,1)S(1)} async-done(((bf16[128,16,512]{0,2,1:T(8,128)(2,1)}), bf16[128,16,512]{0,2,1:T(8,128)(2,1)S(1)}, u32[]{:S(2)}, u32[]{:S(2)}) %all-to-all-start) | async-done | bytes 2097184 | tf_op jit(solution)/shard_map/all_to_all | solution.py:21
  52.9 2.6 copy.40
  55.5 1.7 fusion.81
  57.2 1.4 copy.41
  58.6 0.6 copy.42
  59.2 21.9 %all-gather.4.cloned.1.call-done = bf16[2048,1024]{1,0:T(8,128)(2,1)} async-done(((bf16[128,1024]{1,0:T(8,128)(2,1)}), bf16[2048,1024]{1,0:T(8,128)(2,1)}) %all-gather.4.cloned.1.call-update) | async-done | bytes 4194320 | tf_op jit(solution)/shard_map/all_gather | solution.py:31
  81.1 2.5 fusion.79
  83.8 203.6 %while.15 = (s32[]{:T(128)}, f32[2048,128]{1,0:T(8,128)}, f32[2048,128]{1,0:T(8,128)}, bf16[4,512,2,128]{3,2,1,0:T(2,128)(2,1)}, s32[4]{0:T(128)S(1)}, /*index=5...) while((s32[]{:T(128)}, f32[2048,128]{1,0:T(8,128)}, ...), condition=%wide.region_4.5_spmd.clone, body=%wide.region_0.4_spmd.clone.sunk | while | flops 2730631680 | bytes 93625120 | solution.py:92
  85.2 1.0 fusion.111
  86.2 8.4 %fusion.112 = (f32[2,512]{1,0:T(2,128)S(1)}, f32[2,512,2048]{2,1,0:T(8,128)}) fusion(pred[512,2048]{1,0:T(8,128)(4,1)S(1)} %fusion.111, bf16[2048,128]{1,0:T(8,128)(2,1)S(1)} %get-tuple-element.284, bf16[2048,2,128]{0,2,1:T(8,128)(2,1)} %get-tuple-element.283, s32[]{:T(128)S(6)} %select_n.41), kind=kOutput, calls=%fused_computation.67.clone.1 | convolution fusion | flops 545261568 | bytes 10227716 | tf_op jit(solution)/shard_map/while/body/eval_jaxpr/sub | solution.py:76
  94.6 4.5 %fusion.110 = f32[512,2,2048]{2,0,1:T(8,128)} fusion(bf16[2048,128]{1,0:T(8,128)(2,1)S(1)} %get-tuple-element.286, bf16[2048,2,128]{0,2,1:T(8,128)(2,1)S(1)} %get-tuple-element.285, s32[]{:T(128)S(6)} %select_n.41), kind=kOutput, calls=%fused_computation.31.clone.1 | convolution fusion | flops 536870912 | bytes 9175044 | tf_op jit(solution)/shard_map/while/body/eval_jaxpr/bhd,td->hbt/dot_general | solution.py:79
  99.1 12.7 %fusion.115 = bf16[1,512,2,128]{3,1,2,0:T(8,128)(2,1)S(1)} fusion(f32[512,2,2048]{2,0,1:T(8,128)} %fusion.110, bf16[2048,128]{1,0:T(8,128)(2,1)S(1)} %get-tuple-element.284, f32[2,512,2048]{2,1,0:T(8,128)} %get-tuple-element.244, f32[2,512]{1,0:T(2,128)S(1)} %get-tuple-element.245), kind=kOutput, calls=%fused_computation.29.clone.1 | convolution fusion | flops 551685120 | bytes 17567744 | tf_op jit(solution)/shard_map/while/body/eval_jaxpr/hbt,td->bhd/dot_general | solution.py:82
  111.8 1.0 copy_dynamic-update-slice_fusion.2
  112.8 6.1 %fusion.114 = f32[2048,128]{1,0:T(8,128)} fusion(f32[2048,128]{1,0:T(8,128)} %get-tuple-element.263, pred[]{:T(512)S(6)} %compare.5, bf16[2048,2,128]{0,2,1:T(8,128)(2,1)S(1)} %get-tuple-element.285, s32[]{:T(128)S(6)} %select_n.41, f32[2,512,2048]{2,1,0:T(8,128)} %get-tuple-element.244, f32[2,512]{1,0:T(2,128)S(1)} %get-tuple-element.245), kind=kOutput, calls=%fused_computation.26.clone.1 | convolution fusion | flops 541589504 | bytes 10752005 | tf_op jit(solution)/shard_map/while/body/eval_jaxpr/hbt,bhd->td/dot_general | solution.py:86
  118.9 15.0 %fusion.113 = f32[2048,128]{1,0:T(8,128)S(1)} fusion(f32[512,2,2048]{2,0,1:T(8,128)} %fusion.110, f32[2048,128]{1,0:T(8,128)S(1)} %copy-done.2, pred[]{:T(512)S(6)} %compare.5, bf16[2048,2,128]{0,2,1:T(8,128)(2,1)} %get-tuple-element.283, s32[]{:T(128)S(6)} %select_n.41, f32[2,512,2048]{2,1,0:T(8,128)} %get-tuple-element.244, ...), kind=kOutput, calls=%fused_computation.27.clone.1 | convolution fusion | flops 552078336 | bytes 35921924 | tf_op jit(solution)/shard_map/while/body/eval_jaxpr/hbt,bhd->td/dot_general | solution.py:85
  133.9 1.0 copy-done.3
  136.1 1.0 fusion.111
  137.1 7.4 %fusion.112 = (f32[2,512]{1,0:T(2,128)S(1)}, f32[2,512,2048]{2,1,0:T(8,128)}) fusion(pred[512,2048]{1,0:T(8,128)(4,1)S(1)} %fusion.111, bf16[2048,128]{1,0:T(8,128)(2,1)S(1)} %get-tuple-element.284, bf16[2048,2,128]{0,2,1:T(8,128)(2,1)} %get-tuple-element.283, s32[]{:T(128)S(6)} %select_n.41), kind=kOutput, calls=%fused_computation.67.clone.1 | convolution fusion | flops 545261568 | bytes 10227716 | tf_op jit(solution)/shard_map/while/body/eval_jaxpr/sub | solution.py:76
  144.5 6.5 %fusion.110 = f32[512,2,2048]{2,0,1:T(8,128)} fusion(bf16[2048,128]{1,0:T(8,128)(2,1)S(1)} %get-tuple-element.286, bf16[2048,2,128]{0,2,1:T(8,128)(2,1)S(1)} %get-tuple-element.285, s32[]{:T(128)S(6)} %select_n.41), kind=kOutput, calls=%fused_computation.31.clone.1 | convolution fusion | flops 536870912 | bytes 9175044 | tf_op jit(solution)/shard_map/while/body/eval_jaxpr/bhd,td->hbt/dot_general | solution.py:79
  151.0 13.0 %fusion.115 = bf16[1,512,2,128]{3,1,2,0:T(8,128)(2,1)S(1)} fusion(f32[512,2,2048]{2,0,1:T(8,128)} %fusion.110, bf16[2048,128]{1,0:T(8,128)(2,1)S(1)} %get-tuple-element.284, f32[2,512,2048]{2,1,0:T(8,128)} %get-tuple-element.244, f32[2,512]{1,0:T(2,128)S(1)} %get-tuple-element.245), kind=kOutput, calls=%fused_computation.29.clone.1 | convolution fusion | flops 551685120 | bytes 17567744 | tf_op jit(solution)/shard_map/while/body/eval_jaxpr/hbt,td->bhd/dot_general | solution.py:82
  164.0 1.0 copy_dynamic-update-slice_fusion.2
  165.0 6.3 %fusion.114 = f32[2048,128]{1,0:T(8,128)} fusion(f32[2048,128]{1,0:T(8,128)} %get-tuple-element.263, pred[]{:T(512)S(6)} %compare.5, bf16[2048,2,128]{0,2,1:T(8,128)(2,1)S(1)} %get-tuple-element.285, s32[]{:T(128)S(6)} %select_n.41, f32[2,512,2048]{2,1,0:T(8,128)} %get-tuple-element.244, f32[2,512]{1,0:T(2,128)S(1)} %get-tuple-element.245), kind=kOutput, calls=%fused_computation.26.clone.1 | convolution fusion | flops 541589504 | bytes 10752005 | tf_op jit(solution)/shard_map/while/body/eval_jaxpr/hbt,bhd->td/dot_general | solution.py:86
  171.2 14.7 %fusion.113 = f32[2048,128]{1,0:T(8,128)S(1)} fusion(f32[512,2,2048]{2,0,1:T(8,128)} %fusion.110, f32[2048,128]{1,0:T(8,128)S(1)} %copy-done.2, pred[]{:T(512)S(6)} %compare.5, bf16[2048,2,128]{0,2,1:T(8,128)(2,1)} %get-tuple-element.283, s32[]{:T(128)S(6)} %select_n.41, f32[2,512,2048]{2,1,0:T(8,128)} %get-tuple-element.244, ...), kind=kOutput, calls=%fused_computation.27.clone.1 | convolution fusion | flops 552078336 | bytes 35921924 | tf_op jit(solution)/shard_map/while/body/eval_jaxpr/hbt,bhd->td/dot_general | solution.py:85
  185.9 1.0 copy-done.3
  188.0 1.0 fusion.111
  189.1 7.4 %fusion.112 = (f32[2,512]{1,0:T(2,128)S(1)}, f32[2,512,2048]{2,1,0:T(8,128)}) fusion(pred[512,2048]{1,0:T(8,128)(4,1)S(1)} %fusion.111, bf16[2048,128]{1,0:T(8,128)(2,1)S(1)} %get-tuple-element.284, bf16[2048,2,128]{0,2,1:T(8,128)(2,1)} %get-tuple-element.283, s32[]{:T(128)S(6)} %select_n.41), kind=kOutput, calls=%fused_computation.67.clone.1 | convolution fusion | flops 545261568 | bytes 10227716 | tf_op jit(solution)/shard_map/while/body/eval_jaxpr/sub | solution.py:76
  196.5 4.5 %fusion.110 = f32[512,2,2048]{2,0,1:T(8,128)} fusion(bf16[2048,128]{1,0:T(8,128)(2,1)S(1)} %get-tuple-element.286, bf16[2048,2,128]{0,2,1:T(8,128)(2,1)S(1)} %get-tuple-element.285, s32[]{:T(128)S(6)} %select_n.41), kind=kOutput, calls=%fused_computation.31.clone.1 | convolution fusion | flops 536870912 | bytes 9175044 | tf_op jit(solution)/shard_map/while/body/eval_jaxpr/bhd,td->hbt/dot_general | solution.py:79
  201.0 12.6 %fusion.115 = bf16[1,512,2,128]{3,1,2,0:T(8,128)(2,1)S(1)} fusion(f32[512,2,2048]{2,0,1:T(8,128)} %fusion.110, bf16[2048,128]{1,0:T(8,128)(2,1)S(1)} %get-tuple-element.284, f32[2,512,2048]{2,1,0:T(8,128)} %get-tuple-element.244, f32[2,512]{1,0:T(2,128)S(1)} %get-tuple-element.245), kind=kOutput, calls=%fused_computation.29.clone.1 | convolution fusion | flops 551685120 | bytes 17567744 | tf_op jit(solution)/shard_map/while/body/eval_jaxpr/hbt,td->bhd/dot_general | solution.py:82
  213.6 1.0 copy_dynamic-update-slice_fusion.2
  214.6 6.6 %fusion.114 = f32[2048,128]{1,0:T(8,128)} fusion(f32[2048,128]{1,0:T(8,128)} %get-tuple-element.263, pred[]{:T(512)S(6)} %compare.5, bf16[2048,2,128]{0,2,1:T(8,128)(2,1)S(1)} %get-tuple-element.285, s32[]{:T(128)S(6)} %select_n.41, f32[2,512,2048]{2,1,0:T(8,128)} %get-tuple-element.244, f32[2,512]{1,0:T(2,128)S(1)} %get-tuple-element.245), kind=kOutput, calls=%fused_computation.26.clone.1 | convolution fusion | flops 541589504 | bytes 10752005 | tf_op jit(solution)/shard_map/while/body/eval_jaxpr/hbt,bhd->td/dot_general | solution.py:86
  221.2 14.6 %fusion.113 = f32[2048,128]{1,0:T(8,128)S(1)} fusion(f32[512,2,2048]{2,0,1:T(8,128)} %fusion.110, f32[2048,128]{1,0:T(8,128)S(1)} %copy-done.2, pred[]{:T(512)S(6)} %compare.5, bf16[2048,2,128]{0,2,1:T(8,128)(2,1)} %get-tuple-element.283, s32[]{:T(128)S(6)} %select_n.41, f32[2,512,2048]{2,1,0:T(8,128)} %get-tuple-element.244, ...), kind=kOutput, calls=%fused_computation.27.clone.1 | convolution fusion | flops 552078336 | bytes 35921924 | tf_op jit(solution)/shard_map/while/body/eval_jaxpr/hbt,bhd->td/dot_general | solution.py:85
  235.7 1.0 copy-done.3
  237.9 1.0 fusion.111
  238.9 7.4 %fusion.112 = (f32[2,512]{1,0:T(2,128)S(1)}, f32[2,512,2048]{2,1,0:T(8,128)}) fusion(pred[512,2048]{1,0:T(8,128)(4,1)S(1)} %fusion.111, bf16[2048,128]{1,0:T(8,128)(2,1)S(1)} %get-tuple-element.284, bf16[2048,2,128]{0,2,1:T(8,128)(2,1)} %get-tuple-element.283, s32[]{:T(128)S(6)} %select_n.41), kind=kOutput, calls=%fused_computation.67.clone.1 | convolution fusion | flops 545261568 | bytes 10227716 | tf_op jit(solution)/shard_map/while/body/eval_jaxpr/sub | solution.py:76
  246.4 4.6 %fusion.110 = f32[512,2,2048]{2,0,1:T(8,128)} fusion(bf16[2048,128]{1,0:T(8,128)(2,1)S(1)} %get-tuple-element.286, bf16[2048,2,128]{0,2,1:T(8,128)(2,1)S(1)} %get-tuple-element.285, s32[]{:T(128)S(6)} %select_n.41), kind=kOutput, calls=%fused_computation.31.clone.1 | convolution fusion | flops 536870912 | bytes 9175044 | tf_op jit(solution)/shard_map/while/body/eval_jaxpr/bhd,td->hbt/dot_general | solution.py:79
  251.0 13.7 %fusion.115 = bf16[1,512,2,128]{3,1,2,0:T(8,128)(2,1)S(1)} fusion(f32[512,2,2048]{2,0,1:T(8,128)} %fusion.110, bf16[2048,128]{1,0:T(8,128)(2,1)S(1)} %get-tuple-element.284, f32[2,512,2048]{2,1,0:T(8,128)} %get-tuple-element.244, f32[2,512]{1,0:T(2,128)S(1)} %get-tuple-element.245), kind=kOutput, calls=%fused_computation.29.clone.1 | convolution fusion | flops 551685120 | bytes 17567744 | tf_op jit(solution)/shard_map/while/body/eval_jaxpr/hbt,td->bhd/dot_general | solution.py:82
  264.6 1.0 copy_dynamic-update-slice_fusion.2
  265.6 6.3 %fusion.114 = f32[2048,128]{1,0:T(8,128)} fusion(f32[2048,128]{1,0:T(8,128)} %get-tuple-element.263, pred[]{:T(512)S(6)} %compare.5, bf16[2048,2,128]{0,2,1:T(8,128)(2,1)S(1)} %get-tuple-element.285, s32[]{:T(128)S(6)} %select_n.41, f32[2,512,2048]{2,1,0:T(8,128)} %get-tuple-element.244, f32[2,512]{1,0:T(2,128)S(1)} %get-tuple-element.245), kind=kOutput, calls=%fused_computation.26.clone.1 | convolution fusion | flops 541589504 | bytes 10752005 | tf_op jit(solution)/shard_map/while/body/eval_jaxpr/hbt,bhd->td/dot_general | solution.py:86
  271.9 14.6 %fusion.113 = f32[2048,128]{1,0:T(8,128)S(1)} fusion(f32[512,2,2048]{2,0,1:T(8,128)} %fusion.110, f32[2048,128]{1,0:T(8,128)S(1)} %copy-done.2, pred[]{:T(512)S(6)} %compare.5, bf16[2048,2,128]{0,2,1:T(8,128)(2,1)} %get-tuple-element.283, s32[]{:T(128)S(6)} %select_n.41, f32[2,512,2048]{2,1,0:T(8,128)} %get-tuple-element.244, ...), kind=kOutput, calls=%fused_computation.27.clone.1 | convolution fusion | flops 552078336 | bytes 35921924 | tf_op jit(solution)/shard_map/while/body/eval_jaxpr/hbt,bhd->td/dot_general | solution.py:85
  286.4 1.0 copy-done.3
  287.4 2.0 reshape_reshape.9
  289.4 1.3 convert_bitcast_fusion
  290.6 1.3 convert_bitcast_fusion.1
  292.6 2.9 reduce
  295.6 4.5 %reshape.99 = bf16[16,2,32768]{2,1,0:T(2,128)(2,1)} reshape(bf16[2048,512]{1,0:T(8,128)(2,1)} %reduce) | data formatting | bytes 4194304
  300.1 34.5 %all_to_all.36 = bf16[16,2,32768]{2,1,0:T(2,128)(2,1)S(1)} all-to-all(bf16[16,2,32768]{2,1,0:T(2,128)(2,1)} %reshape.99), channel_id=1, replica_groups=mesh['section'=8,'seq'=16] {'seq'}, dimensions={0} | all-to-all | bytes 4194304 | tf_op jit(solution)/shard_map/all_to_all | solution.py:21
  334.5 6.7 %reshape.100 = bf16[2048,1,512]{2,1,0:T(2,128)(2,1)} reshape(bf16[16,2,32768]{2,1,0:T(2,128)(2,1)S(1)} %all_to_all.36) | data formatting | bytes 4194304
  341.3 2.8 copy.56
  344.7 1.0 copy.48
  345.7 0.7 copy.49
  346.4 4.3 %broadcast_in_dim.36 = bf16[4,4,128,4096]{3,2,1,0:T(8,128)(2,1)S(1)} broadcast(bf16[4,128,4096]{2,1,0:T(8,128)(2,1)} %bitcast.153), dimensions={0,2,3} | broadcast | bytes 20971520 | tf_op jit(solution)/shard_map/broadcast_in_dim | solution.py:112
  350.7 2.4 fusion.82
  353.1 2.1 broadcast_in_dim.37
  355.2 2.4 convolution_add_fusion
  357.6 13.2 %fusion.67 = bf16[128,4096]{1,0:T(8,128)(2,1)S(1)} fusion(f32[128,4096]{1,0:T(8,128)S(1)} %convolution_add_fusion, bf16[128,4096]{0,1:T(8,128)(2,1)S(1)} %bitcast.152, bf16[1,4096,4096]{2,1,0:T(8,128)(2,1)} %all-gather.6.cloned.1.call-done), kind=kOutput, calls=%fused_computation.59 | convolution fusion | flops 4296015872 | bytes 37748736 | tf_op jit(solution)/shard_map/dot_general | solution.py:116
  370.8 3.0 collective-permute-start
  373.8 24.1 %collective-permute-done = bf16[128,4096]{1,0:T(8,128)(2,1)S(1)} collective-permute-done((bf16[128,4096]{1,0:T(8,128)(2,1)S(1)}, bf16[128,4096]{1,0:T(8,128)(2,1)S(1)}, u32[]{:S(2)}, u32[]{:S(2)}) %collective-permute-start) | collective-permute-done | bytes 1048608 | tf_op jit(solution)/shard_map/ppermute | solution.py:38
  397.9 1.0 copy.75
  (44 shorter events, 4.2 us)
Async XLA Ops:
  6.5 74.6 %all-gather.4.cloned.1.call-start = ((), (), s32[]{:S(2)}) async-start(), calls=%async_computation.2 | async-start | bytes 4456448 | tf_op jit(solution)/shard_map/all_gather | solution.py:31
  8.3 349.4 %all-gather.6.cloned.1.call-start = ((), (), s32[]{:S(2)}) async-start(), calls=%async_computation.3 | async-start | bytes 35651584 | tf_op jit(solution)/shard_map/all_gather | solution.py:118
  13.7 39.2 %all-to-all-start = ((bf16[128,16,512]{0,2,1:T(8,128)(2,1)}), bf16[128,16,512]{0,2,1:T(8,128)(2,1)S(1)}, u32[]{:S(2)}, u32[]{:S(2)}) async-start(bf16[128,16,512]{0,2,1:T(8,128)(2,1)} %pad_maximum_fusion), calls=%async_computation | async-start | bytes 4194304 | tf_op jit(solution)/shard_map/all_to_all | solution.py:21
  57.1 26.6 %copy-start.4 = (s32[1,2048]{1,0:T(1,128)S(1)}, s32[1,2048]{1,0:T(1,128)}, u32[]{:S(2)}) copy-start(s32[1,2048]{1,0:T(1,128)} %param.14) | copy-start | bytes 24580
  112.8 6.1 %copy-start.2 = (f32[2048,128]{1,0:T(8,128)S(1)}, f32[2048,128]{1,0:T(8,128)}, u32[]{:S(2)}) copy-start(f32[2048,128]{1,0:T(8,128)} %get-tuple-element.262) | copy-start | bytes 3145732 | tf_op jit(solution)/shard_map/while
  133.9 1.0 copy-start.3
  165.0 6.3 %copy-start.2 = (f32[2048,128]{1,0:T(8,128)S(1)}, f32[2048,128]{1,0:T(8,128)}, u32[]{:S(2)}) copy-start(f32[2048,128]{1,0:T(8,128)} %get-tuple-element.262) | copy-start | bytes 3145732 | tf_op jit(solution)/shard_map/while
  185.9 1.0 copy-start.3
  214.6 6.6 %copy-start.2 = (f32[2048,128]{1,0:T(8,128)S(1)}, f32[2048,128]{1,0:T(8,128)}, u32[]{:S(2)}) copy-start(f32[2048,128]{1,0:T(8,128)} %get-tuple-element.262) | copy-start | bytes 3145732 | tf_op jit(solution)/shard_map/while
  235.7 1.0 copy-start.3
  265.6 6.3 %copy-start.2 = (f32[2048,128]{1,0:T(8,128)S(1)}, f32[2048,128]{1,0:T(8,128)}, u32[]{:S(2)}) copy-start(f32[2048,128]{1,0:T(8,128)} %get-tuple-element.262) | copy-start | bytes 3145732 | tf_op jit(solution)/shard_map/while
  286.4 1.0 copy-start.3
  350.7 2.4 copy-start
  353.1 2.2 copy-start.1
  370.8 27.1 %collective-permute-start = (bf16[128,4096]{1,0:T(8,128)(2,1)S(1)}, bf16[128,4096]{1,0:T(8,128)(2,1)S(1)}, u32[]{:S(2)}, u32[]{:S(2)}) collective-permute-start(bf16[128,4096]{1,0:T(8,128)(2,1)S(1)} %fusion.67), channel_id=1, source_target_pairs={{16,0},{32,16},{48,32},{64,48},{80,64},{96,80},{112,96},{17,1},{33... | collective-permute-start | bytes 3145736 | tf_op jit(solution)/shard_map/ppermute | solution.py:38
Sparse Core Ops, SparseCore 0:
  9.8 71.2 all-gather.3
  83.6 183.3 all-gather.5
where the time goes:
time: 407 us; the launch traced here: 406 us
  matrix products  205 us (50%)
  waiting for transfers between devices  78.7 us (19%)
  local copies, waits for them, and re-layouts  48.7 us (12%)
  blocking collectives  34.5 us (8%)
  between operations  13.7 us (3%)
  other arithmetic  12.9 us (3%)
  starting transfers between devices  10.1 us (2%)
    dot_general x4, matrix products, attend(): jnp.einsum('hbt,bhd->td', dscore, q_blk, preferred_element_type=jnp.float32)  58.8 us
    dot_general x4, matrix products, attend(): jnp.einsum('hbt,td->bhd', dscore, k_head, preferred_element_type=jnp.floa...  52 us
    all_to_all x1, blocking collectives, side_by_side(): lax.all_to_all(both, axis, split_axis=split_dim, concat_axis=concat_dim,...  34.5 us
    all_to_all x1, waiting for transfers between devices, side_by_side(): lax.all_to_all(both, axis, split_axis=split_dim, concat_axis=concat_dim,...  32 us
    sub x4, matrix products, attend(): expo = jnp.exp(scores - top)  30.7 us
    dot_general x4, matrix products, attend(): jnp.einsum('hbt,bhd->td', prob_low, o_blk, preferred_element_type=jnp.flo...  25.2 us
    ppermute x1, waiting for transfers between devices, passed_along(): return lax.ppermute(block, axis, route)  24.1 us
    all_gather x1, waiting for transfers between devices, sent_together(): result = lax.all_gather(both, axis, axis=dim, tiled=True)  21.9 us
  transfers between devices with their start and end apart: 4, of which 3 were waited for; matrix products, arithmetic and copies ran while one was open for 61% of the time, Pallas kernels for 0%

commit v1 on v0

v1 whole, which is shorter than its diff:
```python
import math

import jax
import jax.numpy as jnp
from jax import lax
from jax.experimental import pallas as pl
from jax.experimental.pallas import tpu as pltpu
from jax.sharding import PartitionSpec as P

HD = 128
ROWS = 128
GW = 1024
D = 4096
NC = 8
CW = D // NC
WIN = 9
SCALE = 1.0 / math.sqrt(HD)
NEG = -1e30
MESH = pl.DeviceIdType.MESH
F32 = jnp.float32
BF16 = jnp.bfloat16


def remote(src, dst, send, recv, device):
    return pltpu.make_async_remote_copy(
        src_ref=src, dst_ref=dst, send_sem=send, recv_sem=recv, device_id=device, device_id_type=MESH
    )


def kernel(
    q_ref, k_ref, v_ref, o_ref, doc_ref, w_ref, wk_ref, wv_ref,
    out_ref,
    qs, os_, kv, start, p_s, ds_s, dk, dv, dq, w8, wkv, stage, recv, part, own,
    dkv_s, dkv_c, dkv_o, dkv_i, fin,
    loc, kvz_s, kvz_r, kvy_s, kvy_r, kvc_s, kvc_r, qo_s, qo_r,
    wy_s, wy_r, wc_s, wc_r, wf_s, wf_r, rs_s, rs_r, dc_s, dc_r, dd_s, dd_r, hop_s, hop_r,
):
    sec = lax.axis_index("section")
    seq = lax.axis_index("seq")
    z = seq // 4
    y = lax.rem(seq // 2, 2)
    c = lax.rem(seq, 2)
    yc = y * 2 + c

    def dev(zz, yy, cc):
        return (sec, zz * 4 + yy * 2 + cc)

    def zoff(d):
        return lax.rem(z + d, 4)

    core = dev(z, y, 1 - c)
    ypart = dev(z, 1 - y, c)

    own_q = pltpu.make_async_copy(q_ref.at[:, pl.ds(pl.multiple_of(z * GW, GW), GW)], qs.at[z], loc.at[0])
    own_o = pltpu.make_async_copy(o_ref.at[:, pl.ds(pl.multiple_of(z * GW, GW), GW)], os_.at[z], loc.at[1])
    own_k = pltpu.make_async_copy(
        k_ref.at[:, pl.ds(pl.multiple_of(z * HD, HD), HD)], kv.at[z + 2, yc, :, 0:HD], loc.at[2]
    )
    own_v = pltpu.make_async_copy(
        v_ref.at[:, pl.ds(pl.multiple_of(z * HD, HD), HD)], kv.at[z + 2, yc, :, HD : 2 * HD], loc.at[3]
    )
    own_w = pltpu.make_async_copy(w_ref, w8.at[yc], loc.at[4])
    own_wk = pltpu.make_async_copy(wk_ref, wkv.at[:, 0], loc.at[5])
    own_wv = pltpu.make_async_copy(wv_ref, wkv.at[:, 1], loc.at[6])
    for copy in (own_k, own_v, own_q, own_o, own_w, own_wk, own_wv):
        copy.start()

    barrier = pltpu.get_barrier_semaphore()
    for dy in range(2):
        for dz in range(4):
            if dy or dz:
                pl.semaphore_signal(
                    barrier, inc=1, device_id=dev(zoff(dz), lax.rem(y + dy, 2), c), device_id_type=MESH
                )
    pl.semaphore_signal(barrier, inc=1, device_id=core, device_id_type=MESH)

    @pl.when(sec > 0)
    def _():
        pl.semaphore_signal(barrier, inc=1, device_id=(sec - 1, seq), device_id_type=MESH)

    @pl.when(sec < 7)
    def _():
        pl.semaphore_signal(barrier, inc=1, device_id=(sec + 1, seq), device_id_type=MESH)

    pl.semaphore_wait(barrier, 8 + jnp.where(sec > 0, 1, 0) + jnp.where(sec < 7, 1, 0))

    kv_copies = []
    for d in (1, 3, 2):
        zd = zoff(d)
        cols = pl.ds(pl.multiple_of(zd * HD, HD), HD)
        kv_copies.append(
            (
                remote(k_ref.at[:, cols], kv.at[z + 2, yc, :, 0:HD], kvz_s.at[0, d], kvz_r.at[0, d], dev(zd, y, c)),
                remote(
                    v_ref.at[:, cols], kv.at[z + 2, yc, :, HD : 2 * HD], kvz_s.at[1, d], kvz_r.at[1, d], dev(zd, y, c)
                ),
            )
        )
    for pair in kv_copies:
        pair[0].start()
        pair[1].start()

    def w_y(n):
        cols = pl.ds(n * CW, CW)
        return remote(w_ref.at[:, cols], w8.at[yc, :, cols], wy_s.at[n], wy_r.at[n], ypart)

    def w_y_in(n):
        cols = pl.ds(n * CW, CW)
        at = (1 - y) * 2 + c
        return remote(w_ref.at[:, cols], w8.at[at, :, cols], wy_s.at[n], wy_r.at[n], ypart)

    w_core = remote(w_ref, w8.at[yc], wc_s.at[0], wc_r.at[0], core)

    def w_fwd(n):
        cols = pl.ds(n * CW, CW)
        at = (1 - y) * 2 + c
        return remote(w8.at[at, :, cols], w8.at[at, :, cols], wf_s.at[n], wf_r.at[n], core)

    def w_fwd_in(n):
        cols = pl.ds(n * CW, CW)
        at = (1 - y) * 2 + 1 - c
        return remote(w8.at[at, :, cols], w8.at[at, :, cols], wf_s.at[n], wf_r.at[n], core)

    w_y(0).start()
    qo_copies = []
    for d in (2, 1, 3):
        zd = zoff(d)
        cols = pl.ds(pl.multiple_of(zd * GW, GW), GW)
        qo_copies.append(remote(q_ref.at[:, cols], qs.at[z], qo_s.at[0, d], qo_r.at[0, d], dev(zd, y, c)))
        qo_copies.append(remote(o_ref.at[:, cols], os_.at[z], qo_s.at[1, d], qo_r.at[1, d], dev(zd, y, c)))
    for copy in qo_copies:
        copy.start()
    w_core.start()

    doc = doc_ref[...]
    first = jnp.zeros_like(doc)
    for value in (1, 2, 3):
        before = jnp.sum((doc < value).astype(F32), axis=1, keepdims=True).astype(jnp.int32)
        first = jnp.where(doc == value, before, first)
    start[...] = first
    kv[0:2] = jnp.zeros((2, 4, ROWS, 2 * HD), BF16)
    dk[...] = jnp.zeros_like(dk)
    dv[...] = jnp.zeros_like(dv)

    own_k.wait()
    own_v.wait()
    for d in (1, 3, 2):
        zs = lax.rem(z + 4 - d, 4)
        remote(k_ref.at[:, 0:HD], kv.at[zs + 2, yc, :, 0:HD], kvz_s.at[0, d], kvz_r.at[0, d], core).wait_recv()
        remote(
            v_ref.at[:, 0:HD], kv.at[zs + 2, yc, :, HD : 2 * HD], kvz_s.at[1, d], kvz_r.at[1, d], core
        ).wait_recv()
    kv_y = remote(kv.at[2:6, yc], kv.at[2:6, yc], kvy_s.at[0], kvy_r.at[0], ypart)
    kv_y.start()
    kv_c0 = remote(kv.at[2:6, yc], kv.at[2:6, yc], kvc_s.at[0], kvc_r.at[0], core)
    kv_c0.start()
    for n in range(1, NC):
        w_y(n).start()
    at = (1 - y) * 2 + c
    remote(kv.at[2:6, at], kv.at[2:6, at], kvy_s.at[0], kvy_r.at[0], ypart).wait_recv()
    kv_c1 = remote(kv.at[2:6, at], kv.at[2:6, at], kvc_s.at[1], kvc_r.at[1], core)
    kv_c1.start()
    at = y * 2 + 1 - c
    remote(kv.at[2:6, at], kv.at[2:6, at], kvc_s.at[0], kvc_r.at[0], core).wait_recv()
    at = (1 - y) * 2 + 1 - c
    remote(kv.at[2:6, at], kv.at[2:6, at], kvc_s.at[1], kvc_r.at[1], core).wait_recv()

    kv_rows = kv.reshape(24 * ROWS, 2 * HD)

    def attend(i, carry):
        d = lax.rem(i, 2) * 2 + i // 2
        zb = lax.rem(z + 4 - d, 4)

        @pl.when(d == 0)
        def _():
            own_q.wait()
            own_o.wait()

        @pl.when(d > 0)
        def _():
            remote(q_ref.at[:, 0:GW], qs.at[zb], qo_s.at[0, d], qo_r.at[0, d], core).wait_recv()
            remote(o_ref.at[:, 0:GW], os_.at[zb], qo_s.at[1, d], qo_r.at[1, d], core).wait_recv()

        block = zb * 4 + yc
        at = pl.multiple_of(block * ROWS, ROWS)
        k_win = kv_rows[pl.ds(at, WIN * ROWS), 0:HD]
        base = (block - 8) * ROWS
        lower = start[:, pl.ds(at, ROWS)] - base
        lower = jnp.concatenate([lower, lower], axis=1)

        def heads(hp, carry):
            cols = pl.ds(pl.multiple_of(hp * 2 * HD, 2 * HD), 2 * HD)
            q2 = qs[zb, :, cols]
            q2 = jnp.concatenate([q2[:, 0:HD], q2[:, HD:]], axis=0)
            o2 = os_[zb, :, cols]
            o2 = jnp.concatenate([o2[:, 0:HD], o2[:, HD:]], axis=0)
            v_win = kv_rows[pl.ds(at, WIN * ROWS), HD : 2 * HD]
            k_win = kv_rows[pl.ds(at, WIN * ROWS), 0:HD]
            nt = (((1,), (1,)), ((), ()))
            s = lax.dot_general(k_win, q2, nt, preferred_element_type=F32)
            key = lax.broadcasted_iota(jnp.int32, (8 * ROWS, 2 * ROWS), 0)
            s_a = jnp.where(key >= lower, s[: 8 * ROWS], NEG)
            key = lax.broadcasted_iota(jnp.int32, (ROWS, 2 * ROWS), 0)
            row = lax.broadcasted_iota(jnp.int32, (ROWS, 2 * ROWS), 1)
            row = jnp.where(row >= ROWS, row - ROWS, row)
            s_b = jnp.where((key + 8 * ROWS >= lower) & (key <= row), s[8 * ROWS :], NEG)
            s = jnp.concatenate([s_a, s_b], axis=0)
            top = jnp.max(s, axis=0, keepdims=True)
            e = jnp.exp2((s - top) * (SCALE * math.log2(math.e)))
            inv = 1.0 / jnp.sum(e, axis=0, keepdims=True)
            dp = lax.dot_general(v_win, o2, nt, preferred_element_type=F32)
            delta = jnp.sum(e * dp, axis=0, keepdims=True) * inv
            p_s[:, cols] = (e * inv).astype(BF16)
            ds_s[:, cols] = (e * (dp - delta) * (inv * SCALE)).astype(BF16)
            return carry

        lax.fori_loop(0, 4, heads, 0)
        qb = qs[zb]
        ob = os_[zb]
        qb = jnp.concatenate([qb[:, h * HD : (h + 1) * HD] for h in range(8)], axis=0)
        ob = jnp.concatenate([ob[:, h * HD : (h + 1) * HD] for h in range(8)], axis=0)
        win = pl.ds(at, WIN * ROWS)
        dv[win, :] += jnp.dot(p_s[...], ob, preferred_element_type=F32)
        dk[win, :] += jnp.dot(ds_s[...], qb, preferred_element_type=F32)
        dqt = lax.dot_general(k_win, ds_s[...], (((0,), (0,)), ((), ())), preferred_element_type=F32)
        for h in range(8):
            dq[pl.ds(pl.multiple_of(zb * ROWS, ROWS), ROWS), h * HD : (h + 1) * HD] = dqt[
                :, h * HD : (h + 1) * HD
            ].T.astype(BF16)
        return carry

    lax.fori_loop(0, 4, attend, 0)

    def blocks(b, carry):
        rows = pl.ds(pl.multiple_of((b + 8) * ROWS, ROWS), ROWS)
        dkv_s[b // 4, lax.rem(b, 4), :, 0:HD] = dk[rows, :].astype(BF16)
        dkv_s[b // 4, lax.rem(b, 4), :, HD : 2 * HD] = dv[rows, :].astype(BF16)
        return carry

    lax.fori_loop(0, 16, blocks, 0)
    dc_copies = [
        remote(dkv_s.at[:, yy * 2 + 1 - c], dkv_c.at[yy], dc_s.at[yy], dc_r.at[yy], core) for yy in range(2)
    ]
    for copy in dc_copies:
        copy.start()

    own_w.wait()
    w_core.wait()

    def rs(n, d):
        zd = zoff(d)
        return remote(stage.at[zd, n], recv.at[d - 1, n], rs_s.at[d - 1, n], rs_r.at[d - 1, n], dev(zd, y, c))

    w_y_in(0).wait_recv()
    w_fwd(0).start()

    def product(n, carry):
        cols = pl.ds(pl.multiple_of(n * CW, CW), CW)

        @pl.when(n < NC - 1)
        def _():
            w_y_in(n + 1).wait_recv()
            w_fwd(n + 1).start()

        w_fwd_in(n).wait_recv()
        part[...] = jnp.dot(dq[...], w8.reshape(GW, D)[:, cols], preferred_element_type=F32)
        for zd in range(4):
            stage[zd, n] = part[zd * ROWS : (zd + 1) * ROWS, :].astype(BF16)
        own[:, cols] = part[pl.ds(pl.multiple_of(z * ROWS, ROWS), ROWS), :]
        for d in (2, 1, 3):
            rs(n, d).start()
        return carry

    def dkv_sum():
        for yy in range(2):
            dc_copies[yy].wait_recv()

            def add(zz, carry):
                rows = pl.ds(pl.multiple_of((zz * 4 + yy * 2 + c + 8) * ROWS, ROWS), ROWS)
                dkv_o[yy, zz, :, 0:HD] = (dk[rows, :] + dkv_c[yy, zz, :, 0:HD].astype(F32)).astype(BF16)
                dkv_o[yy, zz, :, HD : 2 * HD] = (dv[rows, :] + dkv_c[yy, zz, :, HD : 2 * HD].astype(F32)).astype(BF16)
                return carry

            lax.fori_loop(0, 4, add, 0)

    def dd(dy, dz):
        yy = lax.rem(y + dy, 2)
        zz = zoff(dz)
        return remote(dkv_o.at[yy, zz], dkv_i.at[y, z], dd_s.at[dy, dz], dd_r.at[dy, dz], dev(zz, yy, c))

    dkv_sum()
    for dy in range(2):
        for dz in range(4):
            if dy or dz:
                dd(dy, dz).start()
    dkv_i[y, z] = dkv_o[y, z]
    lax.fori_loop(0, NC, product, 0)
    own_wk.wait()
    own_wv.wait()
    for dy in range(2):
        for dz in range(4):
            if dy or dz:
                ys = lax.rem(y + dy, 2)
                zs = lax.rem(z + 4 - dz, 4)
                remote(
                    dkv_o.at[ys, zs], dkv_i.at[ys, zs], dd_s.at[dy, dz], dd_r.at[dy, dz], core
                ).wait_recv()

    def hop(n):
        cols = pl.ds(n * CW, CW)
        return remote(fin.at[:, cols], out_ref.at[:, cols], hop_s.at[n], hop_r.at[n], (jnp.maximum(sec - 1, 0), seq))

    def finish(n, carry):
        cols = pl.ds(pl.multiple_of(n * CW, CW), CW)
        dkv = jnp.concatenate(
            [(dkv_i[0, zz].astype(F32) + dkv_i[1, zz].astype(F32)).astype(BF16) for zz in range(4)], axis=1
        )
        total = own[:, cols] + jnp.dot(dkv, wkv.reshape(GW, D)[:, cols], preferred_element_type=F32)
        for d in (1, 3, 2):
            rs(n, d).wait_recv()
            total = total + recv[d - 1, n].astype(F32)
        fin[:, cols] = total.astype(BF16)

        @pl.when(sec > 0)
        def _():
            hop(n).start()

        return carry

    lax.fori_loop(0, NC, finish, 0)

    @pl.when(sec == 7)
    def _():
        out_ref[...] = jnp.zeros_like(out_ref)

    for pair in kv_copies:
        pair[0].wait_send()
        pair[1].wait_send()
    for copy in qo_copies + [kv_y, kv_c0, kv_c1] + dc_copies:
        copy.wait_send()
    for dy in range(2):
        for dz in range(4):
            if dy or dz:
                dd(dy, dz).wait_send()

    def drain(n, carry):
        w_y(n).wait_send()
        w_fwd(n).wait_send()
        for d in (1, 2, 3):
            rs(n, d).wait_send()

        @pl.when(sec > 0)
        def _():
            hop(n).wait_send()

        @pl.when(sec < 7)
        def _():
            hop(n).wait_recv()

        return carry

    lax.fori_loop(0, NC, drain, 0)


def body(queries, keys, values, out_grad, documents, query_weight, key_weight, value_weight):
    hbm = pl.BlockSpec(memory_space=pltpu.MemorySpace.HBM)
    vmem = pl.BlockSpec(memory_space=pltpu.VMEM)
    dma = pltpu.SemaphoreType.DMA
    scratch = [
        pltpu.VMEM((4, ROWS, GW), BF16),
        pltpu.VMEM((4, ROWS, GW), BF16),
        pltpu.VMEM((6, 4, ROWS, 2 * HD), BF16),
        pltpu.VMEM((1, 2048), jnp.int32),
        pltpu.VMEM((WIN * ROWS, GW), BF16),
        pltpu.VMEM((WIN * ROWS, GW), BF16),
        pltpu.VMEM((24 * ROWS, HD), F32),
        pltpu.VMEM((24 * ROWS, HD), F32),
        pltpu.VMEM((4 * ROWS, GW), BF16),
        pltpu.VMEM((4, 256, D), BF16),
        pltpu.VMEM((4, 2, HD, D), BF16),
        pltpu.VMEM((4, NC, ROWS, CW), BF16),
        pltpu.VMEM((3, NC, ROWS, CW), BF16),
        pltpu.VMEM((4 * ROWS, CW), F32),
        pltpu.VMEM((ROWS, D), F32),
        pltpu.VMEM((4, 4, ROWS, 2 * HD), BF16),
        pltpu.VMEM((2, 4, ROWS, 2 * HD), BF16),
        pltpu.VMEM((2, 4, ROWS, 2 * HD), BF16),
        pltpu.VMEM((2, 4, ROWS, 2 * HD), BF16),
        pltpu.VMEM((ROWS, D), BF16),
        dma((7,)),
        dma((2, 4)), dma((2, 4)),
        dma((1,)), dma((1,)),
        dma((2,)), dma((2,)),
        dma((2, 4)), dma((2, 4)),
        dma((NC,)), dma((NC,)),
        dma((1,)), dma((1,)),
        dma((NC,)), dma((NC,)),
        dma((3, NC)), dma((3, NC)),
        dma((2,)), dma((2,)),
        dma((2, 4)), dma((2, 4)),
        dma((NC,)), dma((NC,)),
    ]
    out = pl.pallas_call(
        kernel,
        out_shape=jax.ShapeDtypeStruct((ROWS, D), BF16),
        in_specs=[hbm, hbm, hbm, hbm, vmem, hbm, hbm, hbm],
        out_specs=vmem,
        scratch_shapes=scratch,
        compiler_params=pltpu.CompilerParams(
            collective_id=0, has_side_effects=True, vmem_limit_bytes=67043328
        ),
    )(
        queries[0],
        keys[0],
        values[0],
        out_grad[0],
        documents,
        query_weight[0],
        key_weight[0].reshape(4, HD, D),
        value_weight[0].reshape(4, HD, D),
    )
    return out[None]


def solution(mesh):
    in_specs = (
        P("section", "seq", None),
        P("section", "seq", None),
        P("section", "seq", None),
        P("section", "seq", None),
        P("section", None),
        P("section", "seq", None),
        P("section", None, None),
        P("section", None, None),
    )
    out_specs = P("section", "seq", None)
    return jax.shard_map(body, mesh=mesh, in_specs=in_specs, out_specs=out_specs, check_vma=False)
```

time: 407 us -> 125 us (0.31)
  matrix products: 205 us -> 0 us
  Pallas kernels: 0 us -> 122 us
  waiting for transfers between devices: 78.7 us -> 0 us
  local copies, waits for them, and re-layouts: 48.7 us -> 2.29 us
  blocking collectives: 34.5 us -> 0 us
  between operations: 13.7 us -> 0.01 us
  other arithmetic: 12.9 us -> 0 us
  starting transfers between devices: 10.1 us -> 0 us
    dot_general x19 -> x0, matrix products: 174 us -> none  [the longest x4 58.8 us: attend(): jnp.einsum('hbt,bhd->td', dscore, q_blk, preferred_element_type=jnp.float32)]
    pallas_call x0 -> x1, Pallas kernels: none -> 122 us  [body(): pl.pallas_call(kernel, out_shape=jax.ShapeDtypeStruct((ROWS, D), BF16), i...]
    all_to_all x1 -> x0, blocking collectives: 34.5 us -> none  [side_by_side(): lax.all_to_all(both, axis, split_axis=split_dim, concat_axis=concat_dim,...]
    all_to_all x1 -> x0, waiting for transfers between devices: 32 us -> none  [side_by_side(): lax.all_to_all(both, axis, split_axis=split_dim, concat_axis=concat_dim,...]
    sub x4 -> x0, matrix products: 30.7 us -> none  [attend(): expo = jnp.exp(scores - top)]
    ppermute x1 -> x0, waiting for transfers between devices: 24.1 us -> none  [passed_along(): return lax.ppermute(block, axis, route)]
    all_gather x2 -> x0, waiting for transfers between devices: 21.9 us -> none  [the longest x1 21.9 us: sent_together(): result = lax.all_gather(both, axis, axis=dim, tiled=True)]
    unnamed x12 -> x1, local copies, waits for them, and re-layouts: 18.2 us -> 2.29 us
  transfers between devices with their start and end apart: 4 -> 0, of which waited for: 3 -> 0; matrix products, arithmetic and copies ran while one was open for 61% -> 0% of each run, Pallas kernels for 0% -> 0%
where the time goes in v1:
time: 125 us
  Pallas kernels  122 us (98%)
  local copies, waits for them, and re-layouts  2.29 us (2%)
    pallas_call x1, Pallas kernels, body(): pl.pallas_call(kernel, out_shape=jax.ShapeDtypeStruct((ROWS, D), BF16), i...  122 us

profile of v1, /device:TPU:8, one launch (start us, length us, event | category | flops | bytes accessed | tf_op | source)
XLA Modules:
  0.0 124.7 jit_solution(16618832068554793454)
XLA Ops:
  0.0 122.4 %shard_map.82 = bf16[128,4096]{1,0:T(8,128)(2,1)} custom-call(bf16[128,4096]{1,0:T(8,128)(2,1)} %bitcast.12, bf16[128,512]{1,0:T(8,128)(2,1)} %bitcast.14, bf16[128,512]{1,0:T(8,128)(2,1)} %bitcast.15, bf16[128,4096]{1,0:T(8,128)(2,1)} %bitcast.13, s32[1,2048]{1,0:T(1,128)} %doc_ref.1, bf16[256,4096]{1,0:T(8,128)(2,1)} %bitcast.11, ...), custom_call_target="tpu_custom_call" | custom-call | tf_op jit(solution)/shard_map/pallas_call | solution.py:403
  122.4 2.3 %copy.10 = bf16[1,128,4096]{2,1,0:T(8,128)(2,1)} copy(bf16[1,128,4096]{2,1,0:T(8,128)(2,1)} %bitcast.10) | data formatting | bytes 2097152

commit v2 on v1

v2 whole, which is shorter than its diff:
```python
import math

import jax
import jax.numpy as jnp
from jax import lax
from jax.experimental import pallas as pl
from jax.experimental.pallas import tpu as pltpu
from jax.sharding import PartitionSpec as P

HD = 128
ROWS = 128
GW = 1024
D = 4096
NC = 8
CW = D // NC
W_EARLY = 6
LAG = 4
WIN = 9
SCALE = 1.0 / math.sqrt(HD)
NEG = -1e30
MESH = pl.DeviceIdType.MESH
F32 = jnp.float32
BF16 = jnp.bfloat16


def remote(src, dst, send, recv, device):
    return pltpu.make_async_remote_copy(
        src_ref=src, dst_ref=dst, send_sem=send, recv_sem=recv, device_id=device, device_id_type=MESH
    )


def kernel(
    q_ref, k_ref, v_ref, o_ref, doc_ref, w_ref, wk_ref, wv_ref,
    out_ref,
    qs, os_, kv, start, p_s, ds_s, dk, dv, dq, w8, wkv, half_s, half_r, full_s, full_r, part, own,
    dkv_s, dkv_c, dkv_o, dkv_i, fin,
    loc, kvz_s, kvz_r, kvy_s, kvy_r, kvc_s, kvc_r, qo_s, qo_r,
    wy_s, wy_r, wc_s, wc_r, wf_s, wf_r, ra_s, ra_r, rb_s, rb_r, dc_s, dc_r, dd_s, dd_r, hop_s, hop_r,
):
    sec = lax.axis_index("section")
    seq = lax.axis_index("seq")
    z = seq // 4
    y = lax.rem(seq // 2, 2)
    c = lax.rem(seq, 2)
    yc = y * 2 + c

    def dev(zz, yy, cc):
        return (sec, zz * 4 + yy * 2 + cc)

    def zoff(d):
        return lax.rem(z + d, 4)

    core = dev(z, y, 1 - c)
    ypart = dev(z, 1 - y, c)

    own_q = pltpu.make_async_copy(q_ref.at[:, pl.ds(pl.multiple_of(z * GW, GW), GW)], qs.at[z], loc.at[0])
    own_o = pltpu.make_async_copy(o_ref.at[:, pl.ds(pl.multiple_of(z * GW, GW), GW)], os_.at[z], loc.at[1])
    own_k = pltpu.make_async_copy(
        k_ref.at[:, pl.ds(pl.multiple_of(z * HD, HD), HD)], kv.at[z + 2, yc, :, 0:HD], loc.at[2]
    )
    own_v = pltpu.make_async_copy(
        v_ref.at[:, pl.ds(pl.multiple_of(z * HD, HD), HD)], kv.at[z + 2, yc, :, HD : 2 * HD], loc.at[3]
    )
    own_w = pltpu.make_async_copy(w_ref, w8.at[yc], loc.at[4])
    own_wk = pltpu.make_async_copy(wk_ref, wkv.at[:, 0], loc.at[5])
    own_wv = pltpu.make_async_copy(wv_ref, wkv.at[:, 1], loc.at[6])
    barrier = pltpu.get_barrier_semaphore()
    for dy in range(2):
        for dz in range(4):
            if dy or dz:
                pl.semaphore_signal(
                    barrier, inc=1, device_id=dev(zoff(dz), lax.rem(y + dy, 2), c), device_id_type=MESH
                )
    pl.semaphore_signal(barrier, inc=1, device_id=core, device_id_type=MESH)

    @pl.when(sec > 0)
    def _():
        pl.semaphore_signal(barrier, inc=1, device_id=(sec - 1, seq), device_id_type=MESH)

    @pl.when(sec < 7)
    def _():
        pl.semaphore_signal(barrier, inc=1, device_id=(sec + 1, seq), device_id_type=MESH)

    for copy in (own_k, own_v, own_q, own_o, own_w, own_wk, own_wv):
        copy.start()
    doc = doc_ref[...]
    first = jnp.zeros_like(doc)
    for value in (1, 2, 3):
        before = jnp.sum((doc < value).astype(F32), axis=1, keepdims=True).astype(jnp.int32)
        first = jnp.where(doc == value, before, first)
    start[...] = first
    kv[0:2] = jnp.zeros((2, 4, ROWS, 2 * HD), BF16)
    dk[...] = jnp.zeros_like(dk)
    dv[...] = jnp.zeros_like(dv)
    own_k.wait()
    own_v.wait()
    with jax.named_scope("barrier"):
        pl.semaphore_wait(barrier, 8 + jnp.where(sec > 0, 1, 0) + jnp.where(sec < 7, 1, 0))

    kv_copies = []
    for d in (1, 3, 2):
        zd = zoff(d)
        cols = pl.ds(pl.multiple_of(zd * HD, HD), HD)
        kv_copies.append(
            (
                remote(k_ref.at[:, cols], kv.at[z + 2, yc, :, 0:HD], kvz_s.at[0, d], kvz_r.at[0, d], dev(zd, y, c)),
                remote(
                    v_ref.at[:, cols], kv.at[z + 2, yc, :, HD : 2 * HD], kvz_s.at[1, d], kvz_r.at[1, d], dev(zd, y, c)
                ),
            )
        )
    for pair in kv_copies:
        pair[0].start()
        pair[1].start()

    def kv_y(d):
        zs = lax.rem(z + 4 - d, 4) + 2
        return remote(kv.at[zs, yc], kv.at[zs, yc], kvy_s.at[d], kvy_r.at[d], ypart)

    def kv_y_in(d):
        zs = lax.rem(z + 4 - d, 4) + 2
        at = (1 - y) * 2 + c
        return remote(kv.at[zs, at], kv.at[zs, at], kvy_s.at[d], kvy_r.at[d], ypart)

    def kv_c(i, d):
        zs = lax.rem(z + 4 - d, 4) + 2
        at = yc if i == 0 else (1 - y) * 2 + c
        return remote(kv.at[zs, at], kv.at[zs, at], kvc_s.at[i, d], kvc_r.at[i, d], core)

    def kv_c_in(i, d):
        zs = lax.rem(z + 4 - d, 4) + 2
        at = (y if i == 0 else 1 - y) * 2 + 1 - c
        return remote(kv.at[zs, at], kv.at[zs, at], kvc_s.at[i, d], kvc_r.at[i, d], core)

    def w_y(n):
        cols = pl.ds(n * CW, CW)
        return remote(w_ref.at[:, cols], w8.at[yc, :, cols], wy_s.at[n], wy_r.at[n], ypart)

    def w_y_in(n):
        cols = pl.ds(n * CW, CW)
        at = (1 - y) * 2 + c
        return remote(w_ref.at[:, cols], w8.at[at, :, cols], wy_s.at[n], wy_r.at[n], ypart)

    w_core = remote(w_ref, w8.at[yc], wc_s.at[0], wc_r.at[0], core)

    def w_fwd(n):
        cols = pl.ds(n * CW, CW)
        at = (1 - y) * 2 + c
        return remote(w8.at[at, :, cols], w8.at[at, :, cols], wf_s.at[n], wf_r.at[n], core)

    def w_fwd_in(n):
        cols = pl.ds(n * CW, CW)
        at = (1 - y) * 2 + 1 - c
        return remote(w8.at[at, :, cols], w8.at[at, :, cols], wf_s.at[n], wf_r.at[n], core)

    qo_copies = {}
    for d in (1, 3, 2):
        zd = zoff(d)
        cols = pl.ds(pl.multiple_of(zd * GW, GW), GW)
        qo_copies[d] = (
            remote(q_ref.at[:, cols], qs.at[z], qo_s.at[0, d], qo_r.at[0, d], dev(zd, y, c)),
            remote(o_ref.at[:, cols], os_.at[z], qo_s.at[1, d], qo_r.at[1, d], dev(zd, y, c)),
        )

    kv_y(0).start()
    kv_c(0, 0).start()
    with jax.named_scope("kvz"):
        for d in (1, 3, 2):
            zs = lax.rem(z + 4 - d, 4)
            remote(k_ref.at[:, 0:HD], kv.at[zs + 2, yc, :, 0:HD], kvz_s.at[0, d], kvz_r.at[0, d], core).wait_recv()
            remote(
                v_ref.at[:, 0:HD], kv.at[zs + 2, yc, :, HD : 2 * HD], kvz_s.at[1, d], kvz_r.at[1, d], core
            ).wait_recv()
            kv_y(d).start()
            kv_c(0, d).start()
    for d in (1, 3, 2):
        for copy in qo_copies[d]:
            copy.start()
    with jax.named_scope("kvy"):
        for d in (0, 1, 3, 2):
            kv_y_in(d).wait_recv()
            kv_c(1, d).start()
    for n in range(W_EARLY):
        w_y(n).start()
    w_core.start()
    with jax.named_scope("kvc"):
        for i in range(2):
            for d in range(4):
                kv_c_in(i, d).wait_recv()

    kv_rows = kv.reshape(24 * ROWS, 2 * HD)

    def attend(i, carry):
        d = jnp.where(i == 2, 3, jnp.where(i == 3, 2, i))
        zb = lax.rem(z + 4 - d, 4)

        with jax.named_scope("qowait"):

            @pl.when(d == 0)
            def _():
                own_q.wait()
                own_o.wait()

            @pl.when(d > 0)
            def _():
                remote(q_ref.at[:, 0:GW], qs.at[zb], qo_s.at[0, d], qo_r.at[0, d], core).wait_recv()
                remote(o_ref.at[:, 0:GW], os_.at[zb], qo_s.at[1, d], qo_r.at[1, d], core).wait_recv()

        block = zb * 4 + yc
        at = pl.multiple_of(block * ROWS, ROWS)
        k_win = kv_rows[pl.ds(at, WIN * ROWS), 0:HD]
        base = (block - 8) * ROWS
        lower = start[:, pl.ds(at, ROWS)] - base
        lower = jnp.concatenate([lower, lower], axis=1)

        def heads(hp, carry):
            cols = pl.ds(pl.multiple_of(hp * 2 * HD, 2 * HD), 2 * HD)
            q2 = qs[zb, :, cols]
            q2 = jnp.concatenate([q2[:, 0:HD], q2[:, HD:]], axis=0)
            o2 = os_[zb, :, cols]
            o2 = jnp.concatenate([o2[:, 0:HD], o2[:, HD:]], axis=0)
            v_win = kv_rows[pl.ds(at, WIN * ROWS), HD : 2 * HD]
            k_win = kv_rows[pl.ds(at, WIN * ROWS), 0:HD]
            nt = (((1,), (1,)), ((), ()))
            s = lax.dot_general(k_win, q2, nt, preferred_element_type=F32)
            key = lax.broadcasted_iota(jnp.int32, (8 * ROWS, 2 * ROWS), 0)
            s_a = jnp.where(key >= lower, s[: 8 * ROWS], NEG)
            key = lax.broadcasted_iota(jnp.int32, (ROWS, 2 * ROWS), 0)
            row = lax.broadcasted_iota(jnp.int32, (ROWS, 2 * ROWS), 1)
            row = jnp.where(row >= ROWS, row - ROWS, row)
            s_b = jnp.where((key + 8 * ROWS >= lower) & (key <= row), s[8 * ROWS :], NEG)
            s = jnp.concatenate([s_a, s_b], axis=0)
            top = jnp.max(s, axis=0, keepdims=True)
            e = jnp.exp2((s - top) * (SCALE * math.log2(math.e)))
            inv = 1.0 / jnp.sum(e, axis=0, keepdims=True)
            dp = lax.dot_general(v_win, o2, nt, preferred_element_type=F32)
            delta = jnp.sum(e * dp, axis=0, keepdims=True) * inv
            p_s[:, cols] = (e * inv).astype(BF16)
            ds_s[:, cols] = (e * (dp - delta) * (inv * SCALE)).astype(BF16)
            return carry

        with jax.named_scope("heads"):
            lax.fori_loop(0, 4, heads, 0)
        with jax.named_scope("grads"):
            qb = qs[zb]
            ob = os_[zb]
            qb = jnp.concatenate([qb[:, h * HD : (h + 1) * HD] for h in range(8)], axis=0)
            ob = jnp.concatenate([ob[:, h * HD : (h + 1) * HD] for h in range(8)], axis=0)
            win = pl.ds(at, WIN * ROWS)
            dv[win, :] += jnp.dot(p_s[...], ob, preferred_element_type=F32)
            dk[win, :] += jnp.dot(ds_s[...], qb, preferred_element_type=F32)
            dqt = lax.dot_general(k_win, ds_s[...], (((0,), (0,)), ((), ())), preferred_element_type=F32)
            for h in range(8):
                dq[pl.ds(pl.multiple_of(zb * ROWS, ROWS), ROWS), h * HD : (h + 1) * HD] = dqt[
                    :, h * HD : (h + 1) * HD
                ].T.astype(BF16)
        return carry

    lax.fori_loop(0, 4, attend, 0)

    def blocks(b, carry):
        rows = pl.ds(pl.multiple_of((b * 2 + 1 - c + 8) * ROWS, ROWS), ROWS)
        at = lax.rem(b, 2)
        dkv_s[at, b // 2, :, 0:HD] = dk[rows, :].astype(BF16)
        dkv_s[at, b // 2, :, HD : 2 * HD] = dv[rows, :].astype(BF16)
        return carry

    lax.fori_loop(0, 8, blocks, 0)
    dkv_core = remote(dkv_s, dkv_c, dc_s.at[0], dc_r.at[0], core)
    dkv_core.start()

    with jax.named_scope("wcore"):
        own_w.wait()
        w_core.wait()

    def dd(dy, dz):
        yy = lax.rem(y + dy, 2)
        zz = zoff(dz)
        return remote(dkv_o.at[yy, zz], dkv_i.at[y, z], dd_s.at[dy, dz], dd_r.at[dy, dz], dev(zz, yy, c))

    up, down = dev(zoff(1), y, c), dev(zoff(3), y, c)

    def half(i, n):
        return remote(half_s.at[i, n], half_r.at[i, n], ra_s.at[i, n], ra_r.at[i, n], up if i == 0 else down)

    def full(i, n):
        return remote(full_s.at[i, n], full_r.at[i, n], rb_s.at[i, n], rb_r.at[i, n], up if i == 0 else down)

    def product(n):
        cols = pl.ds(pl.multiple_of(n * CW, CW), CW)
        slot = lax.rem(n, 2)

        with jax.named_scope("prodwait"):

            @pl.when(n < NC - 1)
            def _():
                w_y_in(n + 1).wait_recv()
                w_fwd(n + 1).start()

            w_fwd_in(n).wait_recv()
        with jax.named_scope("proddot"):
            part[slot] = jnp.dot(dq[...], w8.reshape(GW, D)[:, cols], preferred_element_type=F32)
            own[:, cols] = part[slot, pl.ds(pl.multiple_of(z * ROWS, ROWS), ROWS), :]
            rows = pl.ds(pl.multiple_of(zoff(2) * ROWS, ROWS), ROWS)
            for i in range(2):
                half_s[i, n] = part[slot, rows, i * (CW // 2) : (i + 1) * (CW // 2)].astype(BF16)
            for i in range(2):
                half(i, n).start()

    def merge(n):
        slot = lax.rem(n, 2)
        for i in range(2):
            with jax.named_scope("mergewait"):
                half(i, n).wait_recv()
            rows = pl.ds(pl.multiple_of(zoff(1 if i == 0 else 3) * ROWS, ROWS), ROWS)
            mine = slice(0, CW // 2) if i == 0 else slice(CW // 2, CW)
            rest = slice(CW // 2, CW) if i == 0 else slice(0, CW // 2)
            full_s[i, n, :, mine] = (part[slot, rows, mine] + half_r[i, n].astype(F32)).astype(BF16)
            full_s[i, n, :, rest] = part[slot, rows, rest].astype(BF16)
            full(i, n).start()

    def hop(n):
        cols = pl.ds(n * CW, CW)
        return remote(fin.at[:, cols], out_ref.at[:, cols], hop_s.at[n], hop_r.at[n], (jnp.maximum(sec - 1, 0), seq))

    def finish(n):
        cols = pl.ds(pl.multiple_of(n * CW, CW), CW)
        with jax.named_scope("findot"):
            dkv = jnp.concatenate(
                [(dkv_i[0, zz].astype(F32) + dkv_i[1, zz].astype(F32)).astype(BF16) for zz in range(4)], axis=1
            )
            total = own[:, cols] + jnp.dot(dkv, wkv.reshape(GW, D)[:, cols], preferred_element_type=F32)
        with jax.named_scope("finwait"):
            full(0, n).wait_recv()
            full(1, n).wait_recv()
        total = total + full_r[0, n].astype(F32) + full_r[1, n].astype(F32)
        fin[:, cols] = total.astype(BF16)

        @pl.when(sec > 0)
        def _():
            hop(n).start()

    with jax.named_scope("wy0"):
        w_y_in(0).wait_recv()
    w_fwd(0).start()
    product(0)

    with jax.named_scope("dkvsum"):
        dkv_core.wait_recv()
        for yy in range(2):

            def add(zz, carry):
                rows = pl.ds(pl.multiple_of((zz * 4 + yy * 2 + c + 8) * ROWS, ROWS), ROWS)
                dkv_o[yy, zz, :, 0:HD] = (dk[rows, :] + dkv_c[yy, zz, :, 0:HD].astype(F32)).astype(BF16)
                dkv_o[yy, zz, :, HD : 2 * HD] = (dv[rows, :] + dkv_c[yy, zz, :, HD : 2 * HD].astype(F32)).astype(BF16)
                return carry

            lax.fori_loop(0, 4, add, 0)
    for dy in (1, 0):
        for dz in range(4):
            if dy or dz:
                dd(dy, dz).start()
    dkv_i[y, z] = dkv_o[y, z]
    for n in range(W_EARLY, NC):
        w_y(n).start()
    own_wk.wait()
    own_wv.wait()

    def step(n, carry):
        @pl.when(n < NC)
        def _():
            product(n)

        @pl.when(n <= NC)
        def _():
            merge(n - 1)

        @pl.when(n == LAG)
        def _():
            with jax.named_scope("ddwait"):
                for dy in range(2):
                    for dz in range(4):
                        if dy or dz:
                            ys = lax.rem(y + dy, 2)
                            zs = lax.rem(z + 4 - dz, 4)
                            remote(
                                dkv_o.at[ys, zs], dkv_i.at[ys, zs], dd_s.at[dy, dz], dd_r.at[dy, dz], core
                            ).wait_recv()

        @pl.when(n >= LAG)
        def _():
            finish(n - LAG)

        return carry

    lax.fori_loop(1, NC + LAG, step, 0)

    @pl.when(sec == 7)
    def _():
        out_ref[...] = jnp.zeros_like(out_ref)

    with jax.named_scope("drain"):
        for pair in kv_copies:
            pair[0].wait_send()
            pair[1].wait_send()
        for d in range(4):
            kv_y(d).wait_send()
            kv_c(0, d).wait_send()
            kv_c(1, d).wait_send()
        for d in (1, 2, 3):
            for copy in qo_copies[d]:
                copy.wait_send()
        dkv_core.wait_send()
        for dy in range(2):
            for dz in range(4):
                if dy or dz:
                    dd(dy, dz).wait_send()

        def drain(n, carry):
            w_y(n).wait_send()
            w_fwd(n).wait_send()
            for i in range(2):
                half(i, n).wait_send()
                full(i, n).wait_send()

            @pl.when(sec > 0)
            def _():
                hop(n).wait_send()

            @pl.when(sec < 7)
            def _():
                hop(n).wait_recv()

            return carry

        lax.fori_loop(0, NC, drain, 0)


def body(queries, keys, values, out_grad, documents, query_weight, key_weight, value_weight):
    hbm = pl.BlockSpec(memory_space=pltpu.MemorySpace.HBM)
    vmem = pl.BlockSpec(memory_space=pltpu.VMEM)
    dma = pltpu.SemaphoreType.DMA
    scratch = [
        pltpu.VMEM((4, ROWS, GW), BF16),
        pltpu.VMEM((4, ROWS, GW), BF16),
        pltpu.VMEM((6, 4, ROWS, 2 * HD), BF16),
        pltpu.VMEM((1, 2048), jnp.int32),
        pltpu.VMEM((WIN * ROWS, GW), BF16),
        pltpu.VMEM((WIN * ROWS, GW), BF16),
        pltpu.VMEM((24 * ROWS, HD), F32),
        pltpu.VMEM((24 * ROWS, HD), F32),
        pltpu.VMEM((4 * ROWS, GW), BF16),
        pltpu.VMEM((4, 256, D), BF16),
        pltpu.VMEM((4, 2, HD, D), BF16),
        pltpu.VMEM((2, NC, ROWS, CW // 2), BF16),
        pltpu.VMEM((2, NC, ROWS, CW // 2), BF16),
        pltpu.VMEM((2, NC, ROWS, CW), BF16),
        pltpu.VMEM((2, NC, ROWS, CW), BF16),
        pltpu.VMEM((2, 4 * ROWS, CW), F32),
        pltpu.VMEM((ROWS, D), F32),
        pltpu.VMEM((2, 4, ROWS, 2 * HD), BF16),
        pltpu.VMEM((2, 4, ROWS, 2 * HD), BF16),
        pltpu.VMEM((2, 4, ROWS, 2 * HD), BF16),
        pltpu.VMEM((2, 4, ROWS, 2 * HD), BF16),
        pltpu.VMEM((ROWS, D), BF16),
        dma((7,)),
        dma((2, 4)), dma((2, 4)),
        dma((4,)), dma((4,)),
        dma((2, 4)), dma((2, 4)),
        dma((2, 4)), dma((2, 4)),
        dma((NC,)), dma((NC,)),
        dma((1,)), dma((1,)),
        dma((NC,)), dma((NC,)),
        dma((2, NC)), dma((2, NC)),
        dma((2, NC)), dma((2, NC)),
        dma((1,)), dma((1,)),
        dma((2, 4)), dma((2, 4)),
        dma((NC,)), dma((NC,)),
    ]
    out = pl.pallas_call(
        kernel,
        out_shape=jax.ShapeDtypeStruct((ROWS, D), BF16),
        in_specs=[hbm, hbm, hbm, hbm, vmem, hbm, hbm, hbm],
        out_specs=vmem,
        scratch_shapes=scratch,
        compiler_params=pltpu.CompilerParams(
            collective_id=0, has_side_effects=True, vmem_limit_bytes=67043328
        ),
    )(
        queries[0],
        keys[0],
        values[0],
        out_grad[0],
        documents,
        query_weight[0],
        key_weight[0].reshape(4, HD, D),
        value_weight[0].reshape(4, HD, D),
    )
    return out[None]


def solution(mesh):
    in_specs = (
        P("section", "seq", None),
        P("section", "seq", None),
        P("section", "seq", None),
        P("section", "seq", None),
        P("section", None),
        P("section", "seq", None),
        P("section", None, None),
        P("section", None, None),
    )
    out_specs = P("section", "seq", None)
    return jax.shard_map(body, mesh=mesh, in_specs=in_specs, out_specs=out_specs, check_vma=False)
```

time: 125 us -> 107 us (0.86)
  Pallas kernels: 122 us -> 104 us
    pallas_call x1, Pallas kernels: 122 us -> 104 us  [body(): pl.pallas_call(kernel, out_shape=jax.ShapeDtypeStruct((ROWS, D), BF16), i...]
where the time goes in v2:
time: 107 us
  Pallas kernels  104 us (97%)
  local copies, waits for them, and re-layouts  2.29 us (2%)
    pallas_call x1, Pallas kernels, body(): pl.pallas_call(kernel, out_shape=jax.ShapeDtypeStruct((ROWS, D), BF16), i...  104 us
    unnamed x1, local copies, waits for them, and re-layouts  2.29 us

profile of v2, /device:TPU:8, one launch (start us, length us, event | category | flops | bytes accessed | tf_op | source)
XLA Modules:
  0.0 106.7 jit_solution(3929297968819564606)
XLA Ops:
  0.0 104.4 %shard_map.82 = bf16[128,4096]{1,0:T(8,128)(2,1)} custom-call(bf16[128,4096]{1,0:T(8,128)(2,1)} %bitcast.12, bf16[128,512]{1,0:T(8,128)(2,1)} %bitcast.14, bf16[128,512]{1,0:T(8,128)(2,1)} %bitcast.15, bf16[128,4096]{1,0:T(8,128)(2,1)} %bitcast.13, s32[1,2048]{1,0:T(1,128)} %doc_ref.1, bf16[256,4096]{1,0:T(8,128)(2,1)} %bitcast.11, ...), custom_call_target="tpu_custom_call" | custom-call | tf_op jit(solution)/shard_map/pallas_call | solution.py:480
  104.4 2.3 %copy.10 = bf16[1,128,4096]{2,1,0:T(8,128)(2,1)} copy(bf16[1,128,4096]{2,1,0:T(8,128)(2,1)} %bitcast.10) | data formatting | bytes 2097152
